TPU v7x, 8 devices: a whole 2x2x1 slice. The times are simulated.
8 devices in a mesh: fsdp: 2 (over z, y), ep: 4 (over x, core).
Axes of the slice: x: 2, y: 2, z: 1, core: 2. Of those that a mesh axis runs over, the one named last changes fastest.
Arguments:
- grad_out: bfloat16 [8192, 1536], P(('fsdp', 'ep'))
- expert_idx: int32 [8192, 8], P(('fsdp', 'ep'))
- slot_pos: int32 [8192, 8], P(('fsdp', 'ep'))
- gates: float32 [8192, 8], P(('fsdp', 'ep'))
- x_disp: bfloat16 [40, 2048, 1536], P('ep', 'fsdp')
- h_gate: bfloat16 [40, 2048, 512], P('ep', 'fsdp')
- h_up: bfloat16 [40, 2048, 512], P('ep', 'fsdp')
- y_disp: bfloat16 [40, 2048, 1536], P('ep', 'fsdp')
- w_gate: bfloat16 [40, 1536, 512], P('ep', 'fsdp')
- w_down: bfloat16 [40, 512, 1536], P('ep', 'fsdp')
- w_up: bfloat16 [40, 1536, 512], P('ep', 'fsdp')
Outputs:
- output 1: bfloat16 [8192, 1536], P(('fsdp', 'ep'))
- output 2: float32 [8192, 8], P(('fsdp', 'ep'))
- output 3: float32 [40, 1536, 512], P('ep', 'fsdp')
- output 4: float32 [40, 512, 1536], P('ep', 'fsdp')
- output 5: float32 [40, 1536, 512], P('ep', 'fsdp')
All inputs are finite; a program needn't handle non-finite values.
Results may differ from a plain program's by a relative error of at most 0.00111.
Values are sent between devices in bfloat16 or wider.
A program may use at most 1 GiB of HBM per device.

v0:
```python
import jax
import jax.numpy as jnp
from jax import lax
from jax.sharding import PartitionSpec as P


def expert_grads(dy_rows, gate_rows, x_rows, h_gate, h_up, y_rows, w_gate, w_down, w_up):
    g_rows = (dy_rows.astype(jnp.float32) * gate_rows[..., None]).astype(jnp.bfloat16)
    gate_pre = h_gate.astype(jnp.float32)
    up_pre = h_up.astype(jnp.float32)
    sigmoid_gate = jax.nn.sigmoid(gate_pre)
    silu_gate = gate_pre * sigmoid_gate
    act_rows = (silu_gate * up_pre).astype(jnp.bfloat16)
    d_act = jnp.einsum('erd,efd->erf', g_rows, w_down, preferred_element_type=jnp.float32)
    dh_gate = (d_act * up_pre * sigmoid_gate * (1.0 + gate_pre * (1.0 - sigmoid_gate))).astype(jnp.bfloat16)
    dh_up = (d_act * silu_gate).astype(jnp.bfloat16)
    dx_rows = (jnp.einsum('erf,edf->erd', dh_gate, w_gate, preferred_element_type=jnp.float32) + jnp.einsum('erf,edf->erd', dh_up, w_up, preferred_element_type=jnp.float32)).astype(jnp.bfloat16)
    dgate_rows = jnp.einsum('erd,erd->er', dy_rows, y_rows, preferred_element_type=jnp.float32)
    dw_gate = jnp.einsum('erd,erf->edf', x_rows, dh_gate, preferred_element_type=jnp.float32)
    dw_down = jnp.einsum('erf,erd->efd', act_rows, g_rows, preferred_element_type=jnp.float32)
    dw_up = jnp.einsum('erd,erf->edf', x_rows, dh_up, preferred_element_type=jnp.float32)
    return dx_rows, dgate_rows, dw_gate, dw_down, dw_up


def solution(mesh):
    ep_n = mesh.shape['ep']
    tok_spec = P(('fsdp', 'ep'), None)
    row_spec = P('ep', 'fsdp', None)

    def local_backward(grad_out, expert_idx, slot_pos, gates, x_disp, h_gate, h_up, y_disp, w_gate, w_down, w_up):
        tok_n, top_n = expert_idx.shape
        e_loc, rows_loc, width = x_disp.shape
        slot_cap = rows_loc // ep_n
        slots_n = e_loc * ep_n * slot_cap
        choices = tok_n * top_n
        send_row = jnp.where(slot_pos >= 0, ((expert_idx % e_loc) * ep_n + expert_idx // e_loc) * slot_cap + slot_pos, slots_n).reshape(-1)
        src_choice = jnp.full((slots_n,), choices, jnp.int32).at[send_row].set(jnp.arange(choices, dtype=jnp.int32), mode='drop')
        send_dy = jnp.take(grad_out, src_choice // top_n, axis=0, mode='fill', fill_value=0).reshape(e_loc, ep_n, slot_cap, width)
        send_gate = jnp.take(gates.reshape(-1), src_choice, mode='fill', fill_value=0).reshape(e_loc, ep_n, slot_cap)
        recv_dy = lax.all_to_all(send_dy, 'ep', 1, 1, tiled=True).reshape(e_loc, rows_loc, width)
        recv_gate = lax.all_to_all(send_gate, 'ep', 1, 1, tiled=True).reshape(e_loc, rows_loc)
        full_w_gate = lax.all_gather(w_gate, 'fsdp', axis=1, tiled=True)
        full_w_down = lax.all_gather(w_down, 'fsdp', axis=1, tiled=True)
        full_w_up = lax.all_gather(w_up, 'fsdp', axis=1, tiled=True)
        dx_rows, dgate_rows, dw_gate, dw_down, dw_up = expert_grads(recv_dy, recv_gate, x_disp, h_gate, h_up, y_disp, full_w_gate, full_w_down, full_w_up)
        back_dx = lax.all_to_all(dx_rows.reshape(e_loc, ep_n, slot_cap, width), 'ep', 1, 1, tiled=True).reshape(slots_n, width)
        back_gate = lax.all_to_all(dgate_rows.reshape(e_loc, ep_n, slot_cap), 'ep', 1, 1, tiled=True).reshape(slots_n)
        picked = jnp.take(back_dx, send_row, axis=0, mode='fill', fill_value=0).reshape(tok_n, top_n, width)
        grad_x = jnp.sum(picked.astype(jnp.float32), axis=1).astype(jnp.bfloat16)
        grad_gates = jnp.take(back_gate, send_row, mode='fill', fill_value=0).reshape(tok_n, top_n)
        grad_w_gate = lax.psum_scatter(dw_gate, 'fsdp', scatter_dimension=1, tiled=True)
        grad_w_down = lax.psum_scatter(dw_down, 'fsdp', scatter_dimension=1, tiled=True)
        grad_w_up = lax.psum_scatter(dw_up, 'fsdp', scatter_dimension=1, tiled=True)
        return grad_x, grad_gates, grad_w_gate, grad_w_down, grad_w_up

    return jax.shard_map(local_backward, mesh=mesh, in_specs=(tok_spec, tok_spec, tok_spec, tok_spec, row_spec, row_spec, row_spec, row_spec, row_spec, row_spec, row_spec), out_specs=(tok_spec, tok_spec, row_spec, row_spec, row_spec), check_vma=False)
```

profile of v0, /device:TPU:0, one launch (start us, length us, event | category | flops | bytes accessed | tf_op | source)
XLA Modules:
  0.0 1694.8 jit_solution(5992748557260767179)
XLA Ops:
  7.2 0.0 all-gather.4.cloned.1.call-start
  7.2 0.7 all-gather.4.cloned.1.call-update
  7.9 1.0 fusion.20
  9.0 1.0 copy.95
  10.0 1.3 reshape.96
  11.3 1.8 copy.99
  13.0 1.3 reshape.98
  14.4 0.6 copy-done.5
  15.0 30.5 %scatter_custom_fusion = s32[10240]{0:T(1024)S(1)} fusion(s32[8192]{0:T(1024)S(1)} %bitcast.39, s32[8192]{0:T(1024)S(1)} %iota.3, s32[]{:T(128)} %constant.93.clone.1), kind=kCustom, calls=%fused_computation.57 | custom fusion | bytes 40964 | tf_op jit(solution)/shard_map/scatter | solution.py:37
  45.5 56.8 %gather_fusion.1 = f32[10240]{0:T(1024)S(1)} fusion(f32[8192]{0:T(1024)S(1)} %reshape.98, s32[10240]{0:T(1024)S(1)} %get-tuple-element.34), kind=kCustom, calls=%fused_computation.1 | custom fusion | bytes 122880 | tf_op jit(solution)/shard_map/jit(_take)/gather | solution.py:39
  102.3 0.6 copy.100
  103.0 4.6 all-to-all-start.1
  107.7 46.6 %gather_fusion = bf16[10240,1536]{1,0:T(8,128)(2,1)} fusion(bf16[1024,1536]{1,0:T(8,128)(2,1)S(1)} %copy-done, s32[10240]{0:T(1024)S(1)} %get-tuple-element.35), kind=kCustom, calls=%fused_computation | custom fusion | bytes 62955520 | tf_op jit(solution)/shard_map/jit(_take)/gather | solution.py:38
  154.2 21.6 %copy_select_fusion = bf16[10,4,256,1536]{3,2,0,1:T(8,128)(2,1)} fusion(bf16[10,4,256,1536]{3,2,1,0:T(8,128)(2,1)} %bitcast.34, pred[10,4,256]{2,0,1:T(8,128)(4,1)S(1)} %copy.96), kind=kLoop, calls=%fused_computation.10 | loop fusion | flops 15728640 | bytes 62924800 | tf_op jit(solution)/shard_map/jit(_take)/select_n | solution.py:38
  175.8 9.4 all-to-all-start
  185.2 0.0 all-gather.6.cloned.1.call-start
  185.3 0.7 all-gather.6.cloned.1.call-update
  186.0 0.0 all-gather.8.cloned.1.call-start
  186.0 0.7 all-gather.8.cloned.1.call-update
  186.7 0.2 reduce-scatter.4.cloned.1.call-start
  187.0 338.4 %all-to-all-done = bf16[10,4,256,1536]{3,2,0,1:T(8,128)(2,1)} async-done(((bf16[10,4,256,1536]{3,2,0,1:T(8,128)(2,1)}), bf16[10,4,256,1536]{3,2,0,1:T(8,128)(2,1)}, u32[]{:S(2)}, u32[]{:S(2)}) %all-to-all-start) | async-done | bytes 31457312 | tf_op jit(solution)/shard_map/all_to_all | solution.py:40
  525.4 21.6 %copy.98 = bf16[10,4,256,1536]{3,2,1,0:T(8,128)(2,1)} copy(bf16[10,4,256,1536]{3,2,0,1:T(8,128)(2,1)} %all-to-all-done) | data formatting | bytes 62914560 | tf_op jit(solution)/shard_map/all_to_all | solution.py:40
  547.0 32.7 %fusion.1 = (f32[10,1024]{1,0:T(8,128)}, bf16[10,1024,1536]{2,1,0:T(8,128)(2,1)}) fusion(bf16[10,1024,1536]{2,1,0:T(8,128)(2,1)} %param.18, bf16[10,4,256,1536]{3,2,1,0:T(8,128)(2,1)} %copy.98, f32[10,1024]{1,0:T(8,128)S(1)} %bitcast.37), kind=kLoop, calls=%fused_computation.8 | loop fusion | flops 94361600 | bytes 94453760 | tf_op jit(solution)/shard_map/erd,erd->er/dot_general | solution.py:18
  579.6 38.4 %fusion.5 = (bf16[10,1024,512]{2,1,0:T(8,128)(2,1)}, f32[10,1024,512]{2,1,0:T(8,128)}) fusion(bf16[10,1024,512]{2,1,0:T(8,128)(2,1)} %param.17, bf16[10,1024,512]{2,1,0:T(8,128)(2,1)} %param.16, bf16[10,1024,1536]{2,1,0:T(8,128)(2,1)} %get-tuple-element.33, bf16[10,512,1536]{2,1,0:T(8,128)(2,1)} %all-gather.4.cloned.1.call-done), kind=kOutput, calls=%fused_computation.20 | convolution fusion | flops 16169041920 | bytes 99614720 | tf_op jit(solution)/shard_map/erd,efd->erf/dot_general | solution.py:14
  618.1 31.8 %convolution_bitcast_fusion.1 = f32[10,1536,512]{1,2,0:T(8,128)} fusion(bf16[10,1024,512]{2,1,0:T(8,128)(2,1)} %get-tuple-element.36, bf16[10,1024,1536]{2,1,0:T(8,128)(2,1)} %param.15), kind=kOutput, calls=%fused_computation.28 | convolution fusion | flops 16106127360 | bytes 73400320 | tf_op jit(solution)/shard_map/erd,erf->edf/dot_general | solution.py:19
  649.8 0.3 reduce-scatter.8.cloned.1.call-start
  650.1 36.2 %convolution_bitcast_fusion = f32[10,1536,512]{1,2,0:T(8,128)} fusion(bf16[10,1024,1536]{2,1,0:T(8,128)(2,1)} %param.15, f32[10,1024,512]{2,1,0:T(8,128)} %get-tuple-element.37, bf16[10,1024,512]{2,1,0:T(8,128)(2,1)} %param.16), kind=kOutput, calls=%fused_computation.27 | convolution fusion | flops 16142827520 | bytes 94371840 | tf_op jit(solution)/shard_map/erd,erf->edf/dot_general | solution.py:21
  686.3 0.0 reduce-scatter.6.cloned.1.call-start
  686.4 38.5 %fusion.11 = f32[10,512,1536]{2,1,0:T(8,128)} fusion(bf16[10,1024,1536]{2,1,0:T(8,128)(2,1)} %get-tuple-element.33, bf16[10,1024,512]{2,1,0:T(8,128)(2,1)} %param.17, bf16[10,1024,512]{2,1,0:T(8,128)(2,1)} %param.16), kind=kOutput, calls=%fused_computation.29 | convolution fusion | flops 16148070400 | bytes 83886080 | tf_op jit(solution)/shard_map/erf,erd->efd/dot_general | solution.py:20
  724.9 0.8 copy-done.4
  725.8 0.6 copy.104
  726.4 3.5 all-to-all-start.3
  730.0 32.9 %fusion.25 = f32[10,1024,1536]{2,1,0:T(8,128)} fusion(bf16[10,1024,512]{2,1,0:T(8,128)(2,1)} %get-tuple-element.36, bf16[10,1536,512]{2,1,0:T(8,128)(2,1)} %all-gather.6.cloned.1.call-done), kind=kOutput, calls=%fused_computation.62 | convolution fusion | flops 16106127360 | bytes 89128960 | tf_op jit(solution)/shard_map/erf,edf->erd/dot_general | solution.py:17
  762.9 46.5 %add_convert_fusion = bf16[10,1024,1536]{2,1,0:T(8,128)(2,1)} fusion(f32[10,1024,1536]{2,1,0:T(8,128)} %fusion.25, bf16[10,1536,512]{2,1,0:T(8,128)(2,1)} %all-gather.8.cloned.1.call-done, f32[10,1024,512]{2,1,0:T(8,128)} %get-tuple-element.37, bf16[10,1024,512]{2,1,0:T(8,128)(2,1)} %param.16), kind=kOutput, calls=%fused_computation.9 | convolution fusion | flops 16174284800 | bytes 141557760 | tf_op jit(solution)/shard_map/erf,edf->erd/dot_general | solution.py:17
  809.4 21.6 %copy.102 = bf16[10,4,256,1536]{3,2,0,1:T(8,128)(2,1)} copy(bf16[10,4,256,1536]{3,2,1,0:T(8,128)(2,1)} %bitcast.35) | data formatting | bytes 62914560 | tf_op jit(solution)/shard_map/reshape | solution.py:46
  831.0 9.4 all-to-all-start.2
  840.5 45.5 %gather_fusion.3 = f32[8192]{0:T(1024)S(1)} fusion(f32[10240]{0:T(1024)S(1)} %bitcast.32, s32[8192]{0:T(1024)S(1)} %broadcast_clamp_fusion.1), kind=kCustom, calls=%fused_computation.3 | custom fusion | bytes 98304 | tf_op jit(solution)/shard_map/jit(_take)/gather | solution.py:50
  886.1 0.3 gather.28
  886.4 0.2 copy.106
  886.5 0.6 broadcast_select_fusion
  887.2 0.3 copy.94
  887.4 293.0 %all-to-all-done.2 = bf16[10,4,256,1536]{3,2,0,1:T(8,128)(2,1)} async-done(((bf16[10,4,256,1536]{3,2,0,1:T(8,128)(2,1)}), bf16[10,4,256,1536]{3,2,0,1:T(8,128)(2,1)}, u32[]{:S(2)}, u32[]{:S(2)}) %all-to-all-start.2) | async-done | bytes 31457312 | tf_op jit(solution)/shard_map/all_to_all | solution.py:46
  1180.4 21.6 %copy.103 = bf16[10,4,256,1536]{3,2,1,0:T(8,128)(2,1)} copy(bf16[10,4,256,1536]{3,2,0,1:T(8,128)(2,1)} %all-to-all-done.2) | data formatting | bytes 62914560 | tf_op jit(solution)/shard_map/all_to_all | solution.py:46
  1202.0 209.0 %gather_fusion.2 = bf16[8192,1536]{1,0:T(8,128)(2,1)} fusion(bf16[10240,1536]{1,0:T(8,128)(2,1)} %bitcast.33, s32[8192]{0:T(1024)S(1)} %broadcast_clamp_fusion.1), kind=kCustom, calls=%fused_computation.2 | custom fusion | bytes 50364416 | tf_op jit(solution)/shard_map/jit(_take)/gather | solution.py:48
  1411.1 23.1 %fusion.2 = bf16[1024,1536]{1,0:T(8,128)(2,1)} fusion(bf16[8192,1536]{1,0:T(8,128)(2,1)} %gather_fusion.2, pred[1024,8]{1,0:T(8,128)(4,1)S(1)} %copy.94), kind=kLoop, calls=%fused_computation.17 | loop fusion | flops 23592960 | bytes 28319744 | tf_op jit(solution)/shard_map/reduce_sum | solution.py:49
  1434.2 15.8 copy.110
  1450.0 15.6 copy.111
  1465.6 222.3 %reduce-scatter.6.cloned.1.call-done = f32[10,256,1536]{2,1,0:T(8,128)} async-done(((f32[10,512,1536]{2,1,0:T(8,128)}), f32[10,256,1536]{2,1,0:T(8,128)}) %reduce-scatter.6.cloned.1.call-update) | async-done | bytes 15728656 | tf_op jit(solution)/shard_map/reduce_scatter | solution.py:52
  (37 shorter events, 0.5 us)
Async XLA Ops:
  7.2 100.5 %copy-start = (bf16[1024,1536]{1,0:T(8,128)(2,1)S(1)}, bf16[1024,1536]{1,0:T(8,128)(2,1)}, u32[]{:S(2)}) copy-start(bf16[1024,1536]{1,0:T(8,128)(2,1)} %param.11) | copy-start | bytes 9437188
  7.2 572.5 %all-gather.4.cloned.1.call-start = ((), (), s32[]{:S(2)}) async-start(), calls=%async_computation.7 | async-start | bytes 23592960 | tf_op jit(solution)/shard_map/all_gather | solution.py:43
  8.9 2.3 copy-start.2
  14.3 0.6 copy-start.5
  103.0 72.9 %all-to-all-start.1 = ((f32[10,4,256]{2,0,1:T(8,128)}), f32[10,4,256]{2,0,1:T(8,128)S(1)}, u32[]{:S(2)}, u32[]{:S(2)}) async-start(f32[10,4,256]{2,0,1:T(8,128)} %copy.100), calls=%async_computation.1 | async-start | bytes 131072 | tf_op jit(solution)/shard_map/all_to_all | solution.py:41
  175.8 349.5 %all-to-all-start = ((bf16[10,4,256,1536]{3,2,0,1:T(8,128)(2,1)}), bf16[10,4,256,1536]{3,2,0,1:T(8,128)(2,1)}, u32[]{:S(2)}, u32[]{:S(2)}) async-start(bf16[10,4,256,1536]{3,2,0,1:T(8,128)(2,1)} %copy_select_fusion), calls=%async_computation | async-start | bytes 62914560 | tf_op jit(solution)/shard_map/all_to_all | solution.py:40
  185.2 544.8 %all-gather.6.cloned.1.call-start = ((), (), s32[]{:S(2)}) async-start(), calls=%async_computation.8 | async-start | bytes 23592960 | tf_op jit(solution)/shard_map/all_gather | solution.py:42
  186.0 577.0 %all-gather.8.cloned.1.call-start = ((), (), s32[]{:S(2)}) async-start(), calls=%async_computation.9 | async-start | bytes 23592960 | tf_op jit(solution)/shard_map/all_gather | solution.py:44
  186.7 1247.5 %reduce-scatter.4.cloned.1.call-start = ((), (), s32[]{:S(2)}) async-start(), calls=%async_computation.10 | async-start | bytes 47185920 | tf_op jit(solution)/shard_map/reduce_scatter | solution.py:51
  649.8 800.1 %reduce-scatter.8.cloned.1.call-start = ((), (), s32[]{:S(2)}) async-start(), calls=%async_computation.12 | async-start | bytes 47185920 | tf_op jit(solution)/shard_map/reduce_scatter | solution.py:53
  686.3 1001.6 %reduce-scatter.6.cloned.1.call-start = ((), (), s32[]{:S(2)}) async-start(), calls=%async_computation.11 | async-start | bytes 47185920 | tf_op jit(solution)/shard_map/reduce_scatter | solution.py:52
  724.9 0.8 copy-start.4
  726.4 104.6 %all-to-all-start.3 = ((f32[10,4,256]{2,0,1:T(8,128)}), f32[10,4,256]{2,0,1:T(8,128)S(1)}, u32[]{:S(2)}, u32[]{:S(2)}) async-start(f32[10,4,256]{2,0,1:T(8,128)} %copy.104), calls=%async_computation.3 | async-start | bytes 131072 | tf_op jit(solution)/shard_map/all_to_all | solution.py:47
  831.0 9.4 copy-start.6
  831.0 349.4 %all-to-all-start.2 = ((bf16[10,4,256,1536]{3,2,0,1:T(8,128)(2,1)}), bf16[10,4,256,1536]{3,2,0,1:T(8,128)(2,1)}, u32[]{:S(2)}, u32[]{:S(2)}) async-start(bf16[10,4,256,1536]{3,2,0,1:T(8,128)(2,1)} %copy.102), calls=%async_computation.2 | async-start | bytes 62914560 | tf_op jit(solution)/shard_map/all_to_all | solution.py:46
  840.4 46.1 %copy-start.3 = (s32[1024,8]{0,1:T(8,128)S(1)}, s32[1024,8]{0,1:T(8,128)}, u32[]{:S(2)}) copy-start(s32[1024,8]{0,1:T(8,128)} %copy-done.2) | copy-start | bytes 98308
  1434.2 253.7 %copy-start.1 = (bf16[1024,1536]{1,0:T(8,128)(2,1)S(1)}, bf16[1024,1536]{1,0:T(8,128)(2,1)}, u32[]{:S(2)}) copy-start(bf16[1024,1536]{1,0:T(8,128)(2,1)} %param.11) | copy-start | bytes 9437188
Sparse Core Ops, SparseCore 0:
  9.5 187.6 all-gather.3
  198.7 184.7 all-gather.5
  385.0 184.8 all-gather.7
  650.0 344.8 reduce-scatter.3
  997.0 344.0 reduce-scatter.7
  1343.8 344.0 reduce-scatter.5
where the time goes:
time: 1700 us; the launch traced here: 1690 us
  waiting for transfers between devices  856 us (50%)
  local copies, waits for them, and re-layouts  494 us (29%)
  matrix products  224 us (13%)
  other arithmetic  79.2 us (5%)
  starting transfers between devices  27.5 us (2%)
    all_to_all x1, waiting for transfers between devices, local_backward(): lax.all_to_all(send_dy, 'ep', 1, 1, tiled=True)  338 us
    all_to_all x1, waiting for transfers between devices, local_backward(): lax.all_to_all(dx_rows.reshape(e_loc, ep_n, slot_cap, width), 'ep', 1, 1,...  293 us
    reduce_scatter x1, waiting for transfers between devices, local_backward(): lax.psum_scatter(dw_down, 'fsdp', scatter_dimension=1, tiled=True)  222 us
    gather x1, local copies, waits for them, and re-layouts, local_backward(): jnp.take(back_dx, send_row, axis=0, mode='fill', fill_value=0)  209 us
    gather x1, local copies, waits for them, and re-layouts, local_backward(): jnp.take(gates.reshape(-1), src_choice, mode='fill', fill_value=0)  56.8 us
    gather x1, local copies, waits for them, and re-layouts, local_backward(): jnp.take(grad_out, src_choice // top_n, axis=0, mode='fill', fill_value=0)  46.6 us
    dot_general x1, matrix products, expert_grads(): jnp.einsum('erf,edf->erd', dh_up, w_up, preferred_element_type=jnp.float32)  46.5 us
    gather x3, local copies, waits for them, and re-layouts, local_backward(): jnp.take(back_gate, send_row, mode='fill', fill_value=0)  46 us
  transfers between devices with their start and end apart: 10, of which 3 were waited for; matrix products, arithmetic and copies ran while one was open for 47% of the time, Pallas kernels for 0%

commit v1 on v0

v1 whole, which is shorter than its diff:
```python
import functools

import jax
import jax.numpy as jnp
from jax import lax
from jax.experimental import pallas as pl
from jax.experimental.pallas import tpu as pltpu
from jax.sharding import PartitionSpec as P


F32 = jnp.float32
BF16 = jnp.bfloat16


def dot(a, b, dims):
    return lax.dot_general(a, b, (dims, ((), ())), preferred_element_type=F32)


def rows_kernel(has_y, has_init, *refs):
    q_ref, dy_ref, meta_ref = refs[:3]
    refs = refs[3:]
    if has_y:
        y_ref, refs = refs[0], refs[1:]
    if has_init:
        init_ref, refs = refs[0], refs[1:]
    hg_ref, hu_ref, w2_ref, w1_ref, w3_ref, dx_ref, dh1_ref, dh3_ref, dw2_ref = refs[:9]
    refs = refs[9:]
    if has_y:
        gg_ref, refs = refs[0], refs[1:]
    (acc_ref,) = refs
    n, e = pl.program_id(0), pl.program_id(1)
    cap, tok = hg_ref.shape[1], dy_ref.shape[1]
    half = acc_ref.shape[1]

    slot = meta_ref[0, 0, 0:1, :].astype(jnp.int32)
    gate = meta_ref[0, 0, 1:2, :]
    hit = lax.broadcasted_iota(jnp.int32, (cap, tok), 0) == slot
    pick = jnp.where(hit, 1.0, 0.0).astype(BF16)
    s = jnp.sum(jnp.where(hit, gate, 0.0), axis=1, keepdims=True)
    dy = dot(pick, dy_ref[0], ((1,), (0,)))
    if has_y:
        gg = jnp.sum(dy * y_ref[0].astype(F32), axis=1, keepdims=True)
        gg_ref[0, 0] = jnp.sum(jnp.where(hit, gg, 0.0), axis=0, keepdims=True)
    g = (dy * s).astype(BF16)
    h1 = hg_ref[0].astype(F32)
    h3 = hu_ref[0].astype(F32)
    sig = jax.nn.sigmoid(h1)
    silu = h1 * sig
    da = dot(g, w2_ref[0], ((1,), (1,)))
    dh1 = (da * h3 * sig * (1.0 + h1 * (1.0 - sig))).astype(BF16)
    dh3 = (da * silu).astype(BF16)
    dh1_ref[0] = dh1
    dh3_ref[0] = dh3
    a = jnp.where(s > 0.0, silu * h3, 0.0)
    a = jnp.where(q_ref[0] == 0, a[:, :half], a[:, half:]).astype(BF16)
    dw2 = dot(a, g, ((0,), (0,)))
    dx = dot(dh1, w1_ref[0], ((1,), (1,))) + dot(dh3, w3_ref[0], ((1,), (1,)))
    back = dot(pick, dx.astype(BF16), ((0,), (0,)))

    @pl.when(e == 0)
    def _():
        dx_ref[0] = back

    @pl.when(e != 0)
    def _():
        dx_ref[0] += back

    @pl.when(n == 0)
    def _():
        acc_ref[e] = dw2

    @pl.when(n != 0)
    def _():
        acc_ref[e] += dw2

    @pl.when(n == pl.num_programs(0) - 1)
    def _():
        if has_init:
            dw2_ref[0] = acc_ref[e] + init_ref[0]
        else:
            dw2_ref[0] = acc_ref[e]


def rows_back(q, dy, meta, y, init, hg, hu, w2, w1, w3):
    blocks, tok, width = dy.shape
    e_loc, rows, ff = hg.shape
    cap = rows // blocks
    wh = w1.shape[1]
    fh = ff // 2
    has_y, has_init = y is not None, init is not None
    last = blocks - 1
    row = lambda n, e, q_ref: (e, n, 0)
    per_e = lambda n, e, q_ref: (e, 0, 0)
    late_e = lambda n, e, q_ref: (jnp.where(n == last, e, 0), 0, 0)
    in_specs = [pl.BlockSpec((1, tok, width), lambda n, e, q_ref: (n, 0, 0)), pl.BlockSpec((1, 1, 2, tok), lambda n, e, q_ref: (n, e, 0, 0))]
    args = [dy, meta]
    if has_y:
        in_specs.append(pl.BlockSpec((1, cap, width), row))
        args.append(y)
    if has_init:
        in_specs.append(pl.BlockSpec((1, fh, width), late_e))
        args.append(init)
    in_specs += [pl.BlockSpec((1, cap, ff), row), pl.BlockSpec((1, cap, ff), row), pl.BlockSpec((1, ff, width), per_e), pl.BlockSpec((1, wh, ff), per_e), pl.BlockSpec((1, wh, ff), per_e)]
    args += [hg, hu, w2, w1, w3]
    out_shape = [jax.ShapeDtypeStruct((blocks, tok, wh), F32), jax.ShapeDtypeStruct((e_loc, rows, ff), BF16), jax.ShapeDtypeStruct((e_loc, rows, ff), BF16), jax.ShapeDtypeStruct((e_loc, fh, width), F32)]
    out_specs = [pl.BlockSpec((1, tok, wh), lambda n, e, q_ref: (n, 0, 0)), pl.BlockSpec((1, cap, ff), row), pl.BlockSpec((1, cap, ff), row), pl.BlockSpec((1, fh, width), late_e)]
    if has_y:
        out_shape.append(jax.ShapeDtypeStruct((blocks, e_loc, 1, tok), F32))
        out_specs.append(pl.BlockSpec((1, 1, 1, tok), lambda n, e, q_ref: (n, e, 0, 0)))
    steps = blocks * e_loc
    flops = 2 * steps * cap * (tok * width + width * ff + fh * width + 2 * wh * ff + tok * wh)
    return pl.pallas_call(
        functools.partial(rows_kernel, has_y, has_init),
        out_shape=out_shape,
        grid_spec=pltpu.PrefetchScalarGridSpec(num_scalar_prefetch=1, grid=(blocks, e_loc), in_specs=in_specs, out_specs=out_specs, scratch_shapes=[pltpu.VMEM((e_loc, fh, width), F32)]),
        compiler_params=pltpu.CompilerParams(dimension_semantics=("arbitrary", "arbitrary"), vmem_limit_bytes=62 * 1024 * 1024),
        cost_estimate=pl.CostEstimate(flops=flops, bytes_accessed=200_000_000, transcendentals=0),
        name="rows_back",
    )(q, *args)


def weights_kernel(q_ref, xo_ref, xp_ref, d1o_ref, d1p_ref, d3o_ref, d3p_ref, *refs):
    w1_ref, w3_ref = refs[-2:]
    xo, xp = xo_ref[0], xp_ref[0]
    over = ((0,), (0,))
    w1_ref[0] = dot(xo, d1o_ref[0], over) + dot(xp, d1p_ref[0], over)
    w3_ref[0] = dot(xo, d3o_ref[0], over) + dot(xp, d3p_ref[0], over)


def weights_back(q, first, x, xp, d1o, d1p, d3o, d3p, prev):
    e_loc, rows, _ = x.shape
    count, _, wh = xp.shape
    ff = d1o.shape[2]
    here = lambda e, q_ref: (e + first, 0, 0)
    in_specs = [pl.BlockSpec((1, rows, wh), lambda e, q_ref: (e + first, 0, q_ref[0])), pl.BlockSpec((1, rows, wh), lambda e, q_ref: (e, 0, 0))] + [pl.BlockSpec((1, rows, ff), here)] * 4
    args = [x, xp, d1o, d1p, d3o, d3p]
    aliases = {}
    if prev is not None:
        in_specs += [pl.BlockSpec(memory_space=pl.ANY)] * 2
        args += list(prev)
        aliases = {7: 0, 8: 1}
    return pl.pallas_call(
        weights_kernel,
        out_shape=[jax.ShapeDtypeStruct((e_loc, wh, ff), F32)] * 2,
        grid_spec=pltpu.PrefetchScalarGridSpec(num_scalar_prefetch=1, grid=(count,), in_specs=in_specs, out_specs=[pl.BlockSpec((1, wh, ff), here)] * 2),
        input_output_aliases=aliases,
        compiler_params=pltpu.CompilerParams(dimension_semantics=("arbitrary",), vmem_limit_bytes=62 * 1024 * 1024),
        cost_estimate=pl.CostEstimate(flops=8 * count * rows * wh * ff, bytes_accessed=count * 12_000_000, transcendentals=0),
        name="weights_back",
    )(q, *args)


def solution(mesh):
    ep_n = mesh.shape['ep']
    tok_spec = P(('fsdp', 'ep'), None)
    row_spec = P('ep', 'fsdp', None)
    swap = [(0, 1), (1, 0)]

    def local_backward(grad_out, expert_idx, slot_pos, gates, x_disp, h_gate, h_up, y_disp, w_gate, w_down, w_up):
        tok_n, _ = expert_idx.shape
        e_loc, rows_loc, width = x_disp.shape
        e_all = e_loc * ep_n
        wh = width // 2
        q_idx = lax.axis_index('fsdp')
        q = q_idx.astype(jnp.int32).reshape(1)

        ids = jnp.arange(e_all, dtype=jnp.int32)[:, None, None]
        idx_t, slot_t, gates_t = expert_idx.T, slot_pos.T, gates.T
        hit = (idx_t[None] == ids) & (slot_t[None] >= 0)
        slot_map = jnp.max(jnp.where(hit, slot_t[None], -1), axis=1).astype(F32)
        gate_map = jnp.sum(jnp.where(hit, gates_t[None], 0.0), axis=1)
        meta = jnp.stack([slot_map, gate_map], axis=1).reshape(ep_n, e_loc, 2, tok_n)

        def across(a):
            return lax.ppermute(a, 'fsdp', swap)

        meta_own = lax.all_to_all(meta, 'ep', 0, 0, tiled=True)
        meta_par = lax.all_to_all(across(meta), 'ep', 0, 0, tiled=True)

        def ep_sum(a):
            p = lax.axis_index('ep')
            for bit in (1, 2):
                far = (p // bit) % 2
                a = a.reshape((-1, 2) + a.shape[1:]) if bit == 1 else a.reshape((2, -1) + a.shape[1:])
                axis = 1 if bit == 1 else 0
                send = lax.dynamic_index_in_dim(a, 1 - far, axis, keepdims=False)
                keep = lax.dynamic_index_in_dim(a, far, axis, keepdims=False)
                got = lax.ppermute(send, 'ep', [(i, i ^ bit) for i in range(ep_n)])
                a = keep + got
            return a.reshape(a.shape[-2:])

        w2_par = across(w_down)
        dy_par1 = across(grad_out)
        hg_par = across(h_gate)
        hu_par = across(h_up)
        cuts = [(0, 4), (4, 8), (8, e_loc)]
        x_par = []
        for lo, hi in cuts:
            part = lax.dynamic_slice(x_disp, (lo, 0, (1 - q_idx) * wh), (hi - lo, rows_loc, wh))
            x_par.append(across(part))

        dy_own = lax.all_gather(grad_out, 'ep', axis=0)
        dy_par = lax.all_gather(dy_par1, 'ep', axis=0)
        w2 = jnp.where(q_idx == 0, jnp.concatenate([w_down, w2_par], axis=1), jnp.concatenate([w2_par, w_down], axis=1))

        dx_own, d1o, d3o, dw2_own, gg = rows_back(q, dy_own, meta_own, y_disp, None, h_gate, h_up, w2, w_gate, w_up)
        dx_own = ep_sum(dx_own)
        gg = lax.all_to_all(gg.reshape(ep_n, e_loc, tok_n), 'ep', 0, 0, tiled=True).reshape(e_all, tok_n)
        dx_par, d1p, d3p, grad_w_down = rows_back(q, dy_par, meta_par, None, dw2_own, hg_par, hu_par, w2, w_gate, w_up)
        dx_par = ep_sum(dx_par)
        mine = dx_own.astype(BF16)
        other = across(dx_par.astype(BF16))
        grad_x = jnp.where(q_idx == 0, jnp.concatenate([mine, other], axis=1), jnp.concatenate([other, mine], axis=1))
        grad_gates = jnp.sum(jnp.where(hit, gg[:, None, :], 0.0), axis=0).T

        prev = None
        for (lo, hi), xp in zip(cuts, x_par):
            prev = weights_back(q, lo, x_disp, xp, d1o, d1p, d3o, d3p, prev)
        grad_w_gate, grad_w_up = prev
        return grad_x, grad_gates, grad_w_gate, grad_w_down, grad_w_up

    return jax.shard_map(local_backward, mesh=mesh, in_specs=(tok_spec, tok_spec, tok_spec, tok_spec, row_spec, row_spec, row_spec, row_spec, row_spec, row_spec, row_spec), out_specs=(tok_spec, tok_spec, row_spec, row_spec, row_spec), check_vma=False)
```

time: 1700 us -> 1260 us (0.74)
  local copies, waits for them, and re-layouts: 494 us -> 37.4 us
  Pallas kernels: 0 us -> 344 us
  matrix products: 224 us -> 0 us
  waiting for transfers between devices: 856 us -> 795 us
  other arithmetic: 79.2 us -> 41.2 us
    ppermute x0 -> x13, waiting for transfers between devices: none -> 732 us  [the longest x9 732 us: across(): return lax.ppermute(a, 'fsdp', swap)]
    all_to_all x4 -> x3, waiting for transfers between devices: 631 us -> 61.8 us  [the longest x1 61.8 us: local_backward(): lax.all_to_all(gg.reshape(ep_n, e_loc, tok_n), 'ep', 0, 0, tiled=True)]
    gather x6 -> x0, local copies, waits for them, and re-layouts: 358 us -> none  [the longest x1 209 us: local_backward(): jnp.take(back_dx, send_row, axis=0, mode='fill', fill_value=0)]
    pallas_call x0 -> x5, Pallas kernels: none -> 344 us  [the longest x2 295 us: rows_back(): pl.pallas_call(functools.partial(rows_kernel, has_y, has_init), out_shape...]
    dot_general x6 -> x0, matrix products: 224 us -> none  [the longest x1 46.5 us: expert_grads(): jnp.einsum('erf,edf->erd', dh_up, w_up, preferred_element_type=jnp.float32)]
    reduce_scatter x3 -> x0, waiting for transfers between devices: 222 us -> none  [the longest x1 222 us: local_backward(): lax.psum_scatter(dw_down, 'fsdp', scatter_dimension=1, tiled=True)]
    all_to_all x4 -> x0, local copies, waits for them, and re-layouts: 43.3 us -> none  [the longest x1 21.6 us: local_backward(): lax.all_to_all(send_dy, 'ep', 1, 1, tiled=True)]
    dot_general x1 -> x0, other arithmetic: 32.7 us -> none  [expert_grads(): jnp.einsum('erd,erd->er', dy_rows, y_rows, preferred_element_type=jnp.flo...]
  transfers between devices with their start and end apart: 10 -> 18, of which waited for: 3 -> 9; matrix products, arithmetic and copies ran while one was open for 47% -> 5% of each run, Pallas kernels for 0% -> 16%
where the time goes in v1:
time: 1260 us
  waiting for transfers between devices  795 us (63%)
  Pallas kernels  344 us (27%)
  other arithmetic  41.2 us (3%)
  local copies, waits for them, and re-layouts  37.4 us (3%)
  starting transfers between devices  26.2 us (2%)
  between operations  14.3 us (1%)
    ppermute x9, waiting for transfers between devices, across(): return lax.ppermute(a, 'fsdp', swap)  732 us
    pallas_call x2, Pallas kernels, rows_back(): pl.pallas_call(functools.partial(rows_kernel, has_y, has_init), out_shape...  295 us
    all_to_all x1, waiting for transfers between devices, local_backward(): lax.all_to_all(gg.reshape(ep_n, e_loc, tok_n), 'ep', 0, 0, tiled=True)  61.8 us
    pallas_call x3, Pallas kernels, weights_back(): pl.pallas_call(weights_kernel, out_shape=[jax.ShapeDtypeStruct((e_loc, wh...  48.8 us
  transfers between devices with their start and end apart: 18, of which 9 were waited for; matrix products, arithmetic and copies ran while one was open for 5% of the time, Pallas kernels for 16%

profile of v1, /device:TPU:0, one launch (start us, length us, event | category | flops | bytes accessed | tf_op | source)
XLA Modules:
  0.0 1257.8 jit_solution(8659484984224438510)
XLA Ops:
  7.2 0.7 all-gather.5.cloned.1.call-update
  8.0 3.4 collective-permute-start.3
  11.3 68.3 %collective-permute-done.3 = bf16[1024,1536]{1,0:T(8,128)(2,1)S(1)} collective-permute-done((bf16[1024,1536]{1,0:T(8,128)(2,1)}, bf16[1024,1536]{1,0:T(8,128)(2,1)S(1)}, u32[]{:S(2)}, u32[]{:S(2)}) %collective-permute-start.3) | collective-permute-done | bytes 3145760 | tf_op jit(solution)/shard_map/ppermute | solution.py:175
  79.6 1.7 copy-done.3
  81.3 1.8 collective-permute-start
  83.1 0.5 select_reduce_fusion.1
  83.9 0.7 select_reduce_fusion.2
  84.8 1.0 pad_maximum_fusion
  86.1 3.5 all-to-all-start
  89.6 1.8 collective-permute-start.5
  91.6 162.1 %collective-permute-done = bf16[10,256,1536]{2,1,0:T(8,128)(2,1)} collective-permute-done((bf16[10,256,1536]{2,1,0:T(8,128)(2,1)}, bf16[10,256,1536]{2,1,0:T(8,128)(2,1)}, u32[]{:S(2)}, u32[]{:S(2)}) %collective-permute-start) | collective-permute-done | bytes 7864352 | tf_op jit(solution)/shard_map/ppermute | solution.py:175
  253.8 17.7 %maximum_select_fusion.refs_6_ = bf16[10,512,1536]{2,1,0:T(8,128)(2,1)} fusion(bf16[10,256,1536]{2,1,0:T(8,128)(2,1)} %collective-permute-done, bf16[10,256,1536]{2,1,0:T(8,128)(2,1)} %param.20, pred[]{:T(512)S(6)} %eq.22), kind=kLoop, calls=%fused_computation | loop fusion | flops 70778880 | bytes 31457280 | tf_op jit(solution)/shard_map/jit(_where)/select_n | solution.py:204
  271.5 3.6 all-to-all-start.1
  275.2 150.5 %rows_back.2 = (f32[4,1024,768]{2,1,0:T(8,128)}, bf16[10,1024,512]{2,1,0:T(8,128)(2,1)}, bf16[10,1024,512]{2,1,0:T(8,128)(2,1)}, f32[10,256,1536]{2,1,0:T(8,128)}, f32[4,10,1,1024]{3,2,1,0:T(1,128)}) custom-call(s32[1]{0:T(128)} %bitcast.refs_0_.q_ref, bf16[4,1024,1536]{2,1,0:T(8,128)(2,1)} %bitcast.37, f32[4,10,2,1024]{3,2,1,0:T(2,128)} %copy-done.4, ...), custom_call_target="tpu_custom_call" | custom-call | flops 88583700480 | bytes 200000000 | tf_op jit(solution)/shard_map/rows_back/pallas_call | solution.py:112
  425.7 59.8 %collective-permute-done.5.refs_4_ = bf16[10,1024,512]{2,1,0:T(8,128)(2,1)} collective-permute-done((bf16[10,1024,512]{2,1,0:T(8,128)(2,1)}, bf16[10,1024,512]{2,1,0:T(8,128)(2,1)}, u32[]{:S(2)}, u32[]{:S(2)}) %collective-permute-start.5) | collective-permute-done | bytes 10485792 | tf_op jit(solution)/shard_map/ppermute | solution.py:175
  485.5 223.1 %collective-permute-done.6.refs_5_ = bf16[10,1024,512]{2,1,0:T(8,128)(2,1)} collective-permute-done((bf16[10,1024,512]{2,1,0:T(8,128)(2,1)}, bf16[10,1024,512]{2,1,0:T(8,128)(2,1)}, u32[]{:S(2)}, u32[]{:S(2)}) %collective-permute-start.6) | collective-permute-done | bytes 10485792 | tf_op jit(solution)/shard_map/ppermute | solution.py:175
  708.6 144.6 %rows_back.3 = (f32[4,1024,768]{2,1,0:T(8,128)}, bf16[10,1024,512]{2,1,0:T(8,128)(2,1)}, bf16[10,1024,512]{2,1,0:T(8,128)(2,1)}, f32[10,256,1536]{2,1,0:T(8,128)}) custom-call(s32[1]{0:T(128)} %bitcast.refs_0_.q_ref, bf16[4,1024,1536]{2,1,0:T(8,128)(2,1)} %bitcast.36, f32[4,10,2,1024]{3,2,1,0:T(2,128)} %copy-done.5, ...), custom_call_target="tpu_custom_call" | custom-call | flops 88583700480 | bytes 200000000 | tf_op jit(solution)/shard_map/rows_back/pallas_call | solution.py:112
  853.2 6.6 dynamic-slice_bitcast_fusion
  859.8 2.1 copy-done.2
  861.9 3.1 dynamic-slice_bitcast_fusion.1
  865.0 9.9 constant_dynamic-slice_fusion
  874.9 1.5 collective-permute-start.12
  876.4 0.5 collective-permute-start.11
  876.9 5.4 bitcast_add_fusion
  882.3 2.7 copy-done
  885.0 1.9 constant_dynamic-slice_fusion.3
  886.8 1.4 collective-permute-start.8
  888.3 0.8 copy.25
  889.2 3.6 all-to-all-start.2
  892.8 3.7 constant_dynamic-slice_fusion.2
  896.5 1.5 collective-permute-start.10
  898.0 61.8 %all-to-all-done.2 = f32[4,10,1024]{2,1,0:T(8,128)S(1)} async-done(((f32[4,10,1024]{2,1,0:T(8,128)}), f32[4,10,1024]{2,1,0:T(8,128)S(1)}, u32[]{:S(2)}, u32[]{:S(2)}) %all-to-all-start.2) | async-done | bytes 163872 | tf_op jit(solution)/shard_map/all_to_all | solution.py:208
  959.9 0.9 select_reduce_fusion
  960.8 5.4 bitcast_add_fusion.1
  966.2 2.6 copy-done.1
  968.8 1.9 constant_dynamic-slice_fusion.4
  970.7 1.4 collective-permute-start.2
  972.1 41.4 %collective-permute-done.12.xp_ref = bf16[4,1024,768]{2,1,0:T(8,128)(2,1)} collective-permute-done((bf16[4,1024,768]{2,1,0:T(8,128)(2,1)}, bf16[4,1024,768]{2,1,0:T(8,128)(2,1)}, u32[]{:S(2)}, u32[]{:S(2)}) %collective-permute-start.12) | collective-permute-done | bytes 6291488 | tf_op jit(solution)/shard_map/ppermute | solution.py:175
  1013.6 18.8 %weights_back.3 = (f32[10,768,512]{2,1,0:T(8,128)}, f32[10,768,512]{2,1,0:T(8,128)}) custom-call(s32[1]{0:T(128)} %bitcast.refs_0_.q_ref, bf16[10,1024,1536]{2,1,0:T(8,128)(2,1)} %xo_ref.5, bf16[4,1024,768]{2,1,0:T(8,128)(2,1)} %collective-permute-done.12.xp_ref, bf16[10,1024,512]{2,1,0:T(8,128)(2,1)} %get-tuple-element.24.d1o_ref, ...), custom_call_target="tpu_custom_call" | custom-call | flops 12884901888 | bytes 48000000 | tf_op jit(solution)/shard_map/weights_back/pallas_call | solution.py:142
  1032.4 4.3 fusion.1
  1036.7 1.5 collective-permute-start.9
  1038.2 110.2 %collective-permute-done.11.xp_ref = bf16[4,1024,768]{2,1,0:T(8,128)(2,1)} collective-permute-done((bf16[4,1024,768]{2,1,0:T(8,128)(2,1)}, bf16[4,1024,768]{2,1,0:T(8,128)(2,1)}, u32[]{:S(2)}, u32[]{:S(2)}) %collective-permute-start.11) | collective-permute-done | bytes 6291488 | tf_op jit(solution)/shard_map/ppermute | solution.py:175
  1148.4 18.8 %weights_back.4 = (f32[10,768,512]{2,1,0:T(8,128)}, f32[10,768,512]{2,1,0:T(8,128)}) custom-call(s32[1]{0:T(128)} %bitcast.refs_0_.q_ref, bf16[10,1024,1536]{2,1,0:T(8,128)(2,1)} %xo_ref.5, bf16[4,1024,768]{2,1,0:T(8,128)(2,1)} %collective-permute-done.11.xp_ref, ...), custom_call_target="tpu_custom_call", output_to_operand_aliasing={{0}: (7, {}), {1}: (8, {})} | custom-call | flops 12884901888 | bytes 48000000 | tf_op jit(solution)/shard_map/weights_back/pallas_call | solution.py:142
  1167.2 48.6 %collective-permute-done.10.xp_ref = bf16[2,1024,768]{2,1,0:T(8,128)(2,1)} collective-permute-done((bf16[2,1024,768]{2,1,0:T(8,128)(2,1)}, bf16[2,1024,768]{2,1,0:T(8,128)(2,1)}, u32[]{:S(2)}, u32[]{:S(2)}) %collective-permute-start.10) | collective-permute-done | bytes 3145760 | tf_op jit(solution)/shard_map/ppermute | solution.py:175
  1215.8 11.2 weights_back.5
  1227.0 3.2 fusion
  1230.1 18.8 %collective-permute-done.9 = bf16[1024,768]{1,0:T(8,128)(2,1)S(1)} collective-permute-done((bf16[1024,768]{1,0:T(8,128)(2,1)}, bf16[1024,768]{1,0:T(8,128)(2,1)S(1)}, u32[]{:S(2)}, u32[]{:S(2)}) %collective-permute-start.9) | collective-permute-done | bytes 1572896 | tf_op jit(solution)/shard_map/ppermute | solution.py:175
  1248.9 2.0 maximum_select_fusion.1
  (44 shorter events, 1.2 us)
Async XLA Ops:
  7.2 75.9 %copy-start.9 = (s32[1024,8]{0,1:T(8,128)S(1)}, s32[1024,8]{0,1:T(8,128)}, u32[]{:S(2)}) copy-start(s32[1024,8]{0,1:T(8,128)} %param.13) | copy-start | bytes 98308
  7.2 75.9 %copy-start.12 = (f32[1024,8]{0,1:T(8,128)S(1)}, f32[1024,8]{0,1:T(8,128)}, u32[]{:S(2)}) copy-start(f32[1024,8]{0,1:T(8,128)} %param.14) | copy-start | bytes 98308
  7.2 75.9 %copy-start.6 = (s32[1024,8]{0,1:T(8,128)S(1)}, s32[1024,8]{0,1:T(8,128)}, u32[]{:S(2)}) copy-start(s32[1024,8]{0,1:T(8,128)} %param.12) | copy-start | bytes 98308
  7.2 268.0 %all-gather.5.cloned.1.call-start = ((), (), s32[]{:S(2)}) async-start(), calls=%async_computation.3 | async-start | bytes 15728640 | tf_op jit(solution)/shard_map/all_gather | solution.py:202
  7.9 700.7 %all-gather.7.cloned.1.call-start = ((), (), s32[]{:S(2)}) async-start(), calls=%async_computation.4 | async-start | bytes 15728640 | tf_op jit(solution)/shard_map/all_gather | solution.py:203
  8.0 71.7 %collective-permute-start.3 = (bf16[1024,1536]{1,0:T(8,128)(2,1)}, bf16[1024,1536]{1,0:T(8,128)(2,1)S(1)}, u32[]{:S(2)}, u32[]{:S(2)}) collective-permute-start(bf16[1024,1536]{1,0:T(8,128)(2,1)} %param.11), channel_id=1, source_target_pairs={{0,4},{4,0},{1,5},{5,1},{2,6},{6,2},{3,7},{7,3}} | collective-permute-start | bytes 9437192 | tf_op jit(solution)/shard_map/ppermute | solution.py:175
  79.6 1.7 copy-start.3
  81.3 172.4 %collective-permute-start = (bf16[10,256,1536]{2,1,0:T(8,128)(2,1)}, bf16[10,256,1536]{2,1,0:T(8,128)(2,1)}, u32[]{:S(2)}, u32[]{:S(2)}) collective-permute-start(bf16[10,256,1536]{2,1,0:T(8,128)(2,1)} %param.20), channel_id=1, source_target_pairs={{0,4},{4,0},{1,5},{5,1},{2,6},{6,2},{3,7},{7,3}} | collective-permute-start | bytes 23592968 | tf_op jit(solution)/shard_map/ppermute | solution.py:175
  83.1 0.8 copy-start.10
  85.8 185.7 %collective-permute-start.4 = (f32[4,10,2,1024]{3,2,1,0:T(2,128)}, f32[4,10,2,1024]{3,2,1,0:T(2,128)}, u32[]{:S(2)}, u32[]{:S(2)}) collective-permute-start(f32[4,10,2,1024]{3,2,1,0:T(2,128)} %pad_maximum_fusion), channel_id=1, source_target_pairs={{0,4},{4,0},{1,5},{5,1},{2,6},{6,2},{3,7},{7,3}} | collective-permute-start | bytes 983048 | tf_op jit(solution)/shard_map/ppermute | solution.py:175
  86.1 185.4 %all-to-all-start = ((f32[4,10,2,1024]{3,2,1,0:T(2,128)}), f32[4,10,2,1024]{3,2,1,0:T(2,128)S(1)}, u32[]{:S(2)}, u32[]{:S(2)}) async-start(f32[4,10,2,1024]{3,2,1,0:T(2,128)} %pad_maximum_fusion), calls=%async_computation | async-start | bytes 655360 | tf_op jit(solution)/shard_map/all_to_all | solution.py:177
  89.6 395.9 %collective-permute-start.5 = (bf16[10,1024,512]{2,1,0:T(8,128)(2,1)}, bf16[10,1024,512]{2,1,0:T(8,128)(2,1)}, u32[]{:S(2)}, u32[]{:S(2)}) collective-permute-start(bf16[10,1024,512]{2,1,0:T(8,128)(2,1)} %refs_4_.1), channel_id=1, source_target_pairs={{0,4},{4,0},{1,5},{5,1},{2,6},{6,2},{3,7},{7,3}} | collective-permute-start | bytes 31457288 | tf_op jit(solution)/shard_map/ppermute | solution.py:175
  91.3 617.2 %collective-permute-start.6 = (bf16[10,1024,512]{2,1,0:T(8,128)(2,1)}, bf16[10,1024,512]{2,1,0:T(8,128)(2,1)}, u32[]{:S(2)}, u32[]{:S(2)}) collective-permute-start(bf16[10,1024,512]{2,1,0:T(8,128)(2,1)} %refs_5_.1), channel_id=1, source_target_pairs={{0,4},{4,0},{1,5},{5,1},{2,6},{6,2},{3,7},{7,3}} | collective-permute-start | bytes 31457288 | tf_op jit(solution)/shard_map/ppermute | solution.py:175
  271.5 3.7 copy-start.4
  271.5 154.2 %all-to-all-start.1 = ((f32[4,10,2,1024]{3,2,1,0:T(2,128)}), f32[4,10,2,1024]{3,2,1,0:T(2,128)S(1)}, u32[]{:S(2)}, u32[]{:S(2)}) async-start(f32[4,10,2,1024]{3,2,1,0:T(2,128)} %collective-permute-done.4), calls=%async_computation.1 | async-start | bytes 655360 | tf_op jit(solution)/shard_map/all_to_all | solution.py:178
  425.7 282.9 %copy-start.5 = (f32[4,10,2,1024]{3,2,1,0:T(2,128)}, f32[4,10,2,1024]{3,2,1,0:T(2,128)S(1)}, u32[]{:S(2)}) copy-start(f32[4,10,2,1024]{3,2,1,0:T(2,128)S(1)} %all-to-all-done.1.refs_2_) | copy-start | bytes 983044
  853.2 8.7 copy-start.2
  859.8 17.1 %collective-permute-start.7 = (f32[2,1024,768]{2,1,0:T(8,128)}, f32[2,1024,768]{2,1,0:T(8,128)}, u32[]{:S(2)}, u32[]{:S(2)}) collective-permute-start(f32[2,1024,768]{2,1,0:T(8,128)} %dynamic-slice_bitcast_fusion), channel_id=1, source_target_pairs={{0,1},{1,0},{2,3},{3,2},{4,5},{5,4},{6,7},{7,6}} | collective-permute-start | bytes 18874376 | tf_op jit(solution)/shard_map/ppermute | solution.py:188
  865.0 95.8 %collective-permute-start.1 = (f32[2,1024,768]{2,1,0:T(8,128)}, f32[2,1024,768]{2,1,0:T(8,128)}, u32[]{:S(2)}, u32[]{:S(2)}) collective-permute-start(f32[2,1024,768]{2,1,0:T(8,128)} %dynamic-slice_bitcast_fusion.1), channel_id=1, source_target_pairs={{0,1},{1,0},{2,3},{3,2},{4,5},{5,4},{6,7},{7,6}} | collective-permute-start | bytes 18874376 | tf_op jit(solution)/shard_map/ppermute | solution.py:188
  874.9 138.7 %collective-permute-start.12 = (bf16[4,1024,768]{2,1,0:T(8,128)(2,1)}, bf16[4,1024,768]{2,1,0:T(8,128)(2,1)}, u32[]{:S(2)}, u32[]{:S(2)}) collective-permute-start(bf16[4,1024,768]{2,1,0:T(8,128)(2,1)} %get-tuple-element.35), channel_id=1, source_target_pairs={{0,4},{4,0},{1,5},{5,1},{2,6},{6,2},{3,7},{7,3}} | collective-permute-start | bytes 18874376 | tf_op jit(solution)/shard_map/ppermute | solution.py:175
  876.4 272.0 %collective-permute-start.11 = (bf16[4,1024,768]{2,1,0:T(8,128)(2,1)}, bf16[4,1024,768]{2,1,0:T(8,128)(2,1)}, u32[]{:S(2)}, u32[]{:S(2)}) collective-permute-start(bf16[4,1024,768]{2,1,0:T(8,128)(2,1)} %get-tuple-element.36), channel_id=1, source_target_pairs={{0,4},{4,0},{1,5},{5,1},{2,6},{6,2},{3,7},{7,3}} | collective-permute-start | bytes 18874376 | tf_op jit(solution)/shard_map/ppermute | solution.py:175
  882.3 2.7 copy-start
  885.0 3.3 copy-start.8
  885.0 74.9 %copy-start.7 = (s32[1024,8]{0,1:T(8,128)S(1)}, s32[1024,8]{0,1:T(8,128)}, u32[]{:S(2)}) copy-start(s32[1024,8]{0,1:T(8,128)} %param.12) | copy-start | bytes 98308
  885.0 74.9 %copy-start.11 = (pred[8,1024]{1,0:T(8,128)(4,1)S(1)}, pred[8,1024]{1,0:T(8,128)(4,1)}, u32[]{:S(2)}) copy-start(pred[8,1024]{1,0:T(8,128)(4,1)} %copy-done.10) | copy-start | bytes 24580
  886.8 145.5 %collective-permute-start.8 = (f32[1,1024,768]{2,1,0:T(8,128)}, f32[1,1024,768]{2,1,0:T(8,128)}, u32[]{:S(2)}, u32[]{:S(2)}) collective-permute-start(f32[1,1024,768]{2,1,0:T(8,128)} %constant_dynamic-slice_fusion.3), channel_id=1, source_target_pairs={{0,2},{1,3},{2,0},{3,1},{4,6},{5,7},{6,4},{7,5}} | collective-permute-start | bytes 9437192 | tf_op jit(solution)/shard_map/ppermute | solution.py:188
  889.2 70.7 %all-to-all-start.2 = ((f32[4,10,1024]{2,1,0:T(8,128)}), f32[4,10,1024]{2,1,0:T(8,128)S(1)}, u32[]{:S(2)}, u32[]{:S(2)}) async-start(f32[4,10,1024]{2,1,0:T(8,128)} %copy.25), calls=%async_computation.2 | async-start | bytes 524288 | tf_op jit(solution)/shard_map/all_to_all | solution.py:208
  896.5 319.3 %collective-permute-start.10 = (bf16[2,1024,768]{2,1,0:T(8,128)(2,1)}, bf16[2,1024,768]{2,1,0:T(8,128)(2,1)}, u32[]{:S(2)}, u32[]{:S(2)}) collective-permute-start(bf16[2,1024,768]{2,1,0:T(8,128)(2,1)} %constant_dynamic-slice_fusion.2), channel_id=1, source_target_pairs={{0,4},{4,0},{1,5},{5,1},{2,6},{6,2},{3,7},{7,3}} | collective-permute-start | bytes 9437192 | tf_op jit(solution)/shard_map/ppermute | solution.py:175
  966.2 2.6 copy-start.1
  970.7 256.3 %collective-permute-start.2 = (f32[1,1024,768]{2,1,0:T(8,128)}, f32[1,1024,768]{2,1,0:T(8,128)}, u32[]{:S(2)}, u32[]{:S(2)}) collective-permute-start(f32[1,1024,768]{2,1,0:T(8,128)} %constant_dynamic-slice_fusion.4), channel_id=1, source_target_pairs={{0,2},{1,3},{2,0},{3,1},{4,6},{5,7},{6,4},{7,5}} | collective-permute-start | bytes 9437192 | tf_op jit(solution)/shard_map/ppermute | solution.py:188
  1036.7 212.2 %collective-permute-start.9 = (bf16[1024,768]{1,0:T(8,128)(2,1)}, bf16[1024,768]{1,0:T(8,128)(2,1)S(1)}, u32[]{:S(2)}, u32[]{:S(2)}) collective-permute-start(bf16[1024,768]{1,0:T(8,128)(2,1)} %fusion.1), channel_id=1, source_target_pairs={{0,4},{4,0},{1,5},{5,1},{2,6},{6,2},{3,7},{7,3}} | collective-permute-start | bytes 4718600 | tf_op jit(solution)/shard_map/ppermute | solution.py:175
Sparse Core Ops, SparseCore 0:
  9.5 82.0 all-gather.4
  93.8 79.3 all-gather.6
